TPU v7x, 128 devices: a whole 4x4x4 slice. The times are simulated.
128 devices in a mesh: day: 16 (over x, y), pair: 8 (over z, core).
Axes of the slice: x: 4, y: 4, z: 4, core: 2. Of those that a mesh axis runs over, the one named last changes fastest.
Arguments:
- correlations: bfloat16 [64, 4096, 2001], P('day', 'pair'), may hold values from -8 to 8
- mask: int32 [64, 4096], P('day', 'pair'), may hold values from 0 to 1, as said below
- counts: int32 [4096], P(('pair', 'day')), may hold values from 1 to 64, as said below
Outputs:
- phase_weighted: float32 [4096, 2001], P(('pair', 'day'))
- linear: float32 [4096, 2001], P(('pair', 'day'))
Inputs may be any that keep to these rules, and one draw needn't show every extreme that they name: `mask`: every pair has a usable correlation on at least one day. counts[p] equals the number of days d with mask[d, p] = 1.
All inputs are finite; a program needn't handle non-finite values.
Results may differ from a plain program's by a relative error of at most 0.00044.
Values may be sent and summed in bfloat16 or wider, within the bound.
A program may use at most 128 MiB of HBM per device.

v0:
```python
import jax
import jax.numpy as jnp
from jax import lax
from jax.sharding import PartitionSpec as P


def copy_for_each(x, axis):
    count = lax.axis_size(axis)
    return lax.all_to_all(jnp.broadcast_to(x[None], (count, *x.shape)), axis, 0, 0, tiled=True)


def of_everyone(x, axis):
    everything = copy_for_each(x, axis)
    return jnp.sum(everything, axis=0)


def together(arrays, axis):
    line, at, finished = (jnp.concatenate([a.reshape(-1) for a in arrays]), 0, [])
    total = of_everyone(line, axis)
    for a in arrays:
        finished.append(total[at : at + a.size].reshape(a.shape))
        at += a.size
    return tuple(finished)


def in_order(tiles, dim):
    lengths = list(tiles.shape[1:])
    lengths[dim] *= tiles.shape[0]
    return jnp.moveaxis(tiles, 0, dim).reshape(lengths)


def collect(x, axis, dim):
    return in_order(copy_for_each(x, axis), dim)


def hilbert_table(lag_count):
    row_index = lax.broadcasted_iota(jnp.int32, (lag_count, lag_count), 0)
    col_index = lax.broadcasted_iota(jnp.int32, (lag_count, lag_count), 1)
    offset = (col_index - row_index) % lag_count
    offset = jnp.where(offset > lag_count // 2, offset - lag_count, offset)
    phase_angle = jnp.pi * offset.astype(jnp.float32) / lag_count
    parity = 1.0 - 2.0 * (offset % 2).astype(jnp.float32)
    sine_safe = jnp.where(offset == 0, 1.0, jnp.sin(phase_angle))
    table = jnp.where(offset == 0, 0.0, (jnp.cos(phase_angle) - parity) / (lag_count * sine_safe))
    return table.astype(jnp.bfloat16)


def stack_terms(pieces, weight, kernel_table):
    day_count, pair_count, lag_count = pieces.shape
    flattened = pieces.reshape(day_count * pair_count, lag_count)
    hilbert = jnp.dot(flattened, kernel_table, preferred_element_type=jnp.float32)
    day_scale = weight[:, None, None]
    real_part = day_scale * pieces.astype(jnp.float32)
    imag_part = day_scale * hilbert.reshape(day_count, pair_count, lag_count)
    inverse = lax.rsqrt(real_part * real_part + imag_part * imag_part + 0.25)
    return (
        jnp.sum(real_part, axis=0),
        jnp.sum(real_part * inverse, axis=0),
        jnp.sum(imag_part * inverse, axis=0),
    )


def shards(correlations, mask, counts):
    masked = correlations * mask[:, :, None].astype(jnp.bfloat16)
    energy = jnp.sum(jnp.square(masked.astype(jnp.float32)), axis=(1, 2))
    used_pairs = jnp.sum(mask, axis=1).astype(jnp.float32)
    energy, used_pairs = together((energy, used_pairs), "pair")
    lag_count = correlations.shape[2]
    weight = lax.rsqrt(energy / (lag_count * jnp.maximum(used_pairs, 1.0)) + 0.1)
    kernel_table = hilbert_table(lag_count)
    groups = lax.axis_size("day")
    owned_rows = correlations.shape[1] // groups
    weights_all = collect(weight, "day", 0)
    blocks = masked.reshape(correlations.shape[0], groups, owned_rows, lag_count)
    linear_sum, phase_real, phase_imag = stack_terms(
        lax.all_to_all(blocks, "day", split_axis=1, concat_axis=0, tiled=True)[:, 0],
        weights_all,
        kernel_table,
    )
    divisor = jnp.maximum(counts.astype(jnp.float32), 1.0)[:, None]
    linear = linear_sum / divisor
    coherence = (phase_real * phase_real + phase_imag * phase_imag) / (divisor * divisor)
    return (linear * coherence, linear)


def solution(mesh):
    placed = (P("day", "pair", None), P("day", "pair"), P(("pair", "day")))
    return jax.shard_map(
        shards,
        mesh=mesh,
        in_specs=placed,
        out_specs=(P(("pair", "day"), None), P(("pair", "day"), None)),
        check_vma=False,
    )
```

profile of v0, /device:TPU:0, one launch (start us, length us, event | category | flops | bytes accessed | tf_op | source)
XLA Modules:
  0.0 230.1 jit_solution(9688433474302730955)
XLA Ops:
  0.6 0.9 fusion.38
  1.5 13.7 %copy.19 = bf16[4,512,2001]{2,1,0:T(8,128)(2,1)} copy(bf16[4,512,2001]{1,0,2:T(4,128)(2,1)} %param.3) | data formatting | bytes 16392192 | tf_op args[0]
  15.3 8.3 %multiply_reduce_fusion.3 = (f32[4]{0:T(128)S(1)}, bf16[4,512,2001]{2,1,0:T(8,128)(2,1)}) fusion(bf16[4,512,2001]{2,1,0:T(8,128)(2,1)} %copy.19, bf16[4,512]{1,0:T(4,128)(2,1)S(1)} %get-tuple-element.9), kind=kLoop, calls=%fused_computation.10 | loop fusion | flops 16392188 | bytes 16396304 | tf_op jit(solution)/shard_map/reduce_sum | solution.py:65
  23.6 0.1 pad_maximum_fusion
  23.7 10.5 %all_to_all.27 = f32[8,1,8]{2,1,0:T(1,128)S(1)} all-to-all(f32[8,1,8]{2,1,0:T(1,128)S(1)} %broadcast_in_dim.9), channel_id=1, replica_groups=mesh['day'=16,'pair'=8] {'pair'}, dimensions={0} | all-to-all | bytes 512 | tf_op jit(solution)/shard_map/all_to_all | solution.py:9
  34.2 0.1 add_rsqrt_fusion.1
  34.3 0.6 broadcast_in_dim.10
  34.9 7.0 %all-to-all-start.1 = ((f32[16,1,4]{2,1,0:T(1,128)}), f32[16,1,4]{2,1,0:T(1,128)S(1)}, u32[]{:S(2)}, u32[]{:S(2)}) async-start(f32[16,1,4]{2,1,0:T(1,128)} %broadcast_in_dim.10), calls=%async_computation.1 | async-start | bytes 16384 | tf_op jit(solution)/shard_map/all_to_all | solution.py:9
  42.0 8.3 %copy.23 = bf16[4,16,32,2001]{3,2,0,1:T(8,128)(2,1)} copy(bf16[4,16,32,2001]{3,2,1,0:T(8,128)(2,1)} %bitcast.23) | data formatting | bytes 16392192 | tf_op jit(solution)/shard_map/reshape | solution.py:74
  50.2 0.0 copy-start
  50.2 0.0 all-to-all-done.1
  50.2 7.4 %all-to-all-start.2 = ((bf16[4,16,32,2001]{3,2,0,1:T(8,128)(2,1)}), bf16[4,16,32,2001]{3,2,0,1:T(8,128)(2,1)}, u32[]{:S(2)}, u32[]{:S(2)}) async-start(bf16[4,16,32,2001]{3,2,0,1:T(8,128)(2,1)} %copy.23), calls=%async_computation.2 | async-start | bytes 16777216 | tf_op jit(solution)/shard_map/all_to_all | solution.py:76
  57.6 0.0 copy-done
  57.7 82.2 %fusion.14.clone.4 = bf16[2001,2001,1]{1,0,2:T(8,128)(2,1)} fusion(), kind=kLoop, calls=%fused_computation.24.clone.clone.clone.clone.1 | loop fusion | flops 132132008 | bytes 8008002 | tf_op jit(solution)/shard_map/reduce_sum | solution.py:58
  139.9 0.5 broadcast.52
  140.4 0.7 reduce.5
  141.1 0.1 mul.76
  141.2 56.9 %all-to-all-done.2 = bf16[4,16,32,2001]{3,2,0,1:T(8,128)(2,1)} async-done(((bf16[4,16,32,2001]{3,2,0,1:T(8,128)(2,1)}), bf16[4,16,32,2001]{3,2,0,1:T(8,128)(2,1)}, u32[]{:S(2)}, u32[]{:S(2)}) %all-to-all-start.2) | async-done | bytes 8196128 | tf_op jit(solution)/shard_map/all_to_all | solution.py:76
  198.1 0.0 copy-start.1
  198.1 5.8 %multiply_reduce_fusion.2 = f32[32,2001]{1,0:T(8,128)S(1)} fusion(bf16[4,16,32,2001]{3,2,0,1:T(8,128)(2,1)} %all-to-all-done.2, f32[16,4]{1,0:T(8,128)S(1)} %bitcast.24), kind=kLoop, calls=%fused_computation.9 | loop fusion | flops 12230112 | bytes 8452480 | tf_op jit(solution)/shard_map/reduce_sum | solution.py:57
  204.0 0.0 copy-done.1
  204.0 25.2 %multiply_reduce_fusion.1 = (f32[32,2001]{1,0:T(8,128)S(1)}, f32[32,2001]{1,0:T(8,128)S(1)}) fusion(f32[64]{0:T(128)S(1)} %mul.76, bf16[4,16,32,2001]{3,2,0,1:T(8,128)(2,1)} %all-to-all-done.2, bf16[64,32,2001]{2,1,0:T(8,128)(2,1)} %bitcast.6, bf16[2001,2001,1]{1,0,2:T(8,128)(2,1)S(1)} %copy-done.1), kind=kOutput, calls=%fused_computation.6 | convolution fusion | flops 16445337600 | bytes 24912706 | tf_op jit(solution)/shard_map/dot_general | solution.py:51
  229.2 0.9 divide_multiply_fusion
  (4 shorter events, 0.0 us)
Async XLA Ops:
  34.9 15.3 %all-to-all-start.1 = ((f32[16,1,4]{2,1,0:T(1,128)}), f32[16,1,4]{2,1,0:T(1,128)S(1)}, u32[]{:S(2)}, u32[]{:S(2)}) async-start(f32[16,1,4]{2,1,0:T(1,128)} %broadcast_in_dim.10), calls=%async_computation.1 | async-start | bytes 16384 | tf_op jit(solution)/shard_map/all_to_all | solution.py:9
  50.2 7.4 %copy-start = (s32[32]{0:T(128)S(1)}, s32[32]{0:T(128)}, u32[]{:S(2)}) copy-start(s32[32]{0:T(128)} %param.5) | copy-start | bytes 388
  50.2 147.9 %all-to-all-start.2 = ((bf16[4,16,32,2001]{3,2,0,1:T(8,128)(2,1)}), bf16[4,16,32,2001]{3,2,0,1:T(8,128)(2,1)}, u32[]{:S(2)}, u32[]{:S(2)}) async-start(bf16[4,16,32,2001]{3,2,0,1:T(8,128)(2,1)} %copy.23), calls=%async_computation.2 | async-start | bytes 16777216 | tf_op jit(solution)/shard_map/all_to_all | solution.py:76
  198.1 5.9 %copy-start.1 = (bf16[2001,2001,1]{1,0,2:T(8,128)(2,1)S(1)}, bf16[2001,2001,1]{1,0,2:T(8,128)(2,1)}, u32[]{:S(2)}) copy-start(bf16[2001,2001,1]{1,0,2:T(8,128)(2,1)} %fusion.14.clone.4) | copy-start | bytes 24024010
where the time goes:
time: 234 us; the launch traced here: 230 us
  other arithmetic  99.1 us (42%)
  waiting for transfers between devices  56.9 us (24%)
  matrix products  25.2 us (11%)
  local copies, waits for them, and re-layouts  23.2 us (10%)
  starting transfers between devices  14.4 us (6%)
  blocking collectives  10.5 us (4%)
    reduce_sum x1, other arithmetic, stack_terms(): jnp.sum(real_part * inverse, axis=0)  82.2 us
    all_to_all x1, waiting for transfers between devices, shards(): lax.all_to_all(blocks, 'day', split_axis=1, concat_axis=0, tiled=True)[:, 0]  56.9 us
    dot_general x1, matrix products, stack_terms(): jnp.dot(flattened, kernel_table, preferred_element_type=jnp.float32)  25.2 us
    unnamed x5, local copies, waits for them, and re-layouts  13.8 us
    all_to_all x1, blocking collectives, copy_for_each(): lax.all_to_all(jnp.broadcast_to(x[None], (count, *x.shape)), axis, 0, 0,...  10.5 us
    reduce_sum x1, other arithmetic, shards(): energy = jnp.sum(jnp.square(masked.astype(jnp.float32)), axis=(1, 2))  8.34 us
    reshape x1, local copies, waits for them, and re-layouts, shards(): masked.reshape(correlations.shape[0], groups, owned_rows, lag_count)  8.25 us
    all_to_all x1, starting transfers between devices, shards(): lax.all_to_all(blocks, 'day', split_axis=1, concat_axis=0, tiled=True)[:, 0]  7.41 us
  transfers between devices with their start and end apart: 2, of which 1 were waited for; matrix products, arithmetic and copies ran while one was open for 40% of the time, Pallas kernels for 0%

commit v1 on v0

v1 whole, which is shorter than its diff:
```python
import jax
import jax.numpy as jnp
from jax import lax
from jax.experimental import pallas as pl
from jax.experimental.pallas import tpu as pltpu
from jax.sharding import PartitionSpec as P

BF = jnp.bfloat16
F32 = jnp.float32
MESH = pl.DeviceIdType.MESH
LAGS = 2001
WIDE = 2048


def alpha(v):
    return v + 1 - 2 * (v % 2)


def beta(v):
    return 3 - v


def hilbert_rows():
    u = lax.broadcasted_iota(jnp.int32, (8, 4096), 1)
    s = lax.broadcasted_iota(jnp.int32, (8, 4096), 0)
    t = jnp.where(u < 3840, u, u - 4096) - 1792 - s
    offset = (t + 4 * LAGS) % LAGS
    offset = jnp.where(offset > LAGS // 2, offset - LAGS, offset)
    phase_angle = jnp.pi * offset.astype(F32) / LAGS
    parity = 1.0 - 2.0 * (offset % 2).astype(F32)
    sine_safe = jnp.where(offset == 0, 1.0, jnp.sin(phase_angle))
    return jnp.where(offset == 0, 0.0, (jnp.cos(phase_angle) - parity) / (LAGS * sine_safe))


def kernel(x_hbm, mask_ref, counts_ref, rows_ref, pw_ref, lin_ref,
           slab, flat, xr, r1, table, s1, s2, r2, r3, r4, en, ww, wn,
           in_sem, a_s, a_r, b_s, b_r, c_s, c_r, d_s, d_r, e_s, e_r, w_s, w_r):
    day = lax.axis_index("day")
    pair = lax.axis_index("pair")
    x = day // 4
    y = day % 4
    xa, xb, ya, yb = alpha(x), beta(x), alpha(y), beta(y)
    x2, y2 = (x + 2) % 4, (y + 2) % 4
    along_x_a, along_x_b = (x, xa, xb, x2), (x, xb, xa, x2)
    along_y_a, along_y_b = (y, ya, yb, y2), (y, yb, ya, y2)
    firsts = (along_x_a, along_x_b, along_y_a, along_y_b)
    seconds = (along_y_a, along_y_b, along_x_a, along_x_b)

    def at_first(c, v):
        return (v * 4 + y, pair) if c < 2 else (x * 4 + v, pair)

    def at_second(c, v):
        return (x * 4 + v, pair) if c < 2 else (v * 4 + y, pair)

    neighbours = [(xa * 4 + y, pair), (xb * 4 + y, pair), (x * 4 + ya, pair), (x * 4 + yb, pair)]
    peers = [(day, (pair + k) % 8) for k in range(1, 8)]

    def load_block(i, cb):
        cols = pl.ds(pl.multiple_of(cb * 128, 128), 128)
        return pltpu.make_async_copy(x_hbm.at[:, :, cols], slab.at[i], in_sem.at[i])

    order = (x2, xa, xb, x)
    loads = [load_block(i, cb) for i, cb in enumerate(order)]
    for load in loads:
        load.start()

    barrier = pltpu.get_barrier_semaphore()
    for to in neighbours + peers:
        pl.semaphore_signal(barrier, inc=1, device_id=to, device_id_type=MESH)

    flat[pl.ds(8000, 192), :] = jnp.zeros((192, 128), F32)

    def remote(src, dst, send, recv, to):
        return pltpu.make_async_remote_copy(
            src_ref=src, dst_ref=dst, send_sem=send, recv_sem=recv, device_id=to, device_id_type=MESH
        )

    def raw_block(c, g, a):
        return remote(xr.at[c, a], r1.at[c, g], a_s.at[c, g], a_r.at[c, g], at_first(c, firsts[c][1]))

    def raw_piece(c, g, a, b):
        return remote(xr.at[c, a, b], r1.at[c, g, b], a_s.at[c, g], a_r.at[c, g], at_first(c, firsts[c][1]))

    squares = jnp.zeros((8, 128), F32)
    used = jnp.zeros((8, 128), F32)
    for i, cb in enumerate(order):
        loads[i].wait()
        cols = pl.ds(pl.multiple_of(cb * 128, 128), 128)
        m4 = mask_ref[:, cols].astype(F32)
        m8 = jnp.concatenate([m4, m4], axis=0)
        used = used + m8
        rows = slab.at[i].reshape(4 * LAGS, 128)

        def widen(j, acc, rows=rows, m8=m8):
            at = pl.ds(pl.multiple_of(j * 32, 32), 32)
            v = rows[at, :].astype(F32).reshape(4, 8, 128) * m8[None]
            flat[at, :] = v.reshape(32, 128)
            return acc + jnp.sum(v * v, axis=0)

        squares = lax.fori_loop(0, 250, widen, squares, unroll=10)
        last = rows[pl.ds(8000, 4), :].astype(F32) * m4
        flat[pl.ds(8000, 4), :] = last
        squares = squares + jnp.concatenate([last * last, jnp.zeros((4, 128), F32)], axis=0)

        def turn(j, carry, cb=cb):
            lags = pl.ds(pl.multiple_of(j * 128, 128), 128)
            for d in range(4):
                t = flat[pl.ds(pl.multiple_of(j * 512, 512) + d, 128, stride=4), :]
                t = t.astype(BF).T.reshape(4, 4, 8, 128)
                for c in range(2):
                    xr[c, cb, :, d, :, lags] = t[:, c]
                for c in range(2, 4):
                    for q in range(4):
                        xr[c, q, cb, d, :, lags] = t[q, c]
            return carry

        lax.fori_loop(0, 16, turn, 0, unroll=2)
        if i == 0:
            pl.semaphore_wait(barrier, len(neighbours) + len(peers))
            for c in range(2):
                raw_block(c, 0, x2).start()
        if i == 1:
            raw_block(0, 1, xa).start()
        if i == 2:
            raw_block(1, 1, xb).start()
        for c in range(2, 4):
            raw_piece(c, 0, y2, cb).start()
    for c in range(2, 4):
        for cb in order:
            raw_piece(c, 1, firsts[c][1], cb).start()

    en[0, 0] = squares
    en[0, 1] = used
    energy_copies = [
        remote(en.at[0], en.at[k], e_s.at[k], e_r.at[k], peers[k - 1]) for k in range(1, 8)
    ]
    for copy in energy_copies:
        copy.start()

    def tabulate(j, carry):
        lo = pltpu.roll(rows_ref[...], j * 16, 1)
        hi = pltpu.roll(rows_ref[...], j * 16 + 8, 1)
        both = jnp.concatenate([lo, hi], axis=0).astype(BF)
        for a in range(8):
            table[pl.ds(pl.multiple_of(a * 256 + j * 16, 16), 16), :] = both[:, 256 * (7 - a) : 256 * (7 - a) + WIDE]
        return carry

    lax.fori_loop(0, 16, tabulate, 0)

    for copy in energy_copies:
        copy.wait_recv()
    total = jnp.sum(en[:, 0], axis=0)
    pairs_used = jnp.sum(en[:, 1], axis=0)
    energy = jnp.sum(total[:4] + total[4:], axis=1, keepdims=True)
    pairs_used = jnp.sum(pairs_used[:4], axis=1, keepdims=True)
    level = energy / (LAGS * jnp.maximum(pairs_used, 1.0)) + 0.1
    weight = lax.rsqrt(level)
    for d in range(4):
        ww[0, d] = jnp.broadcast_to(weight[d : d + 1], (8, 128))
        ww[1, d] = jnp.broadcast_to(0.25 * level[d : d + 1], (8, 128))
    weight_copies = [remote(ww, wn.at[k], w_s.at[k], w_r.at[k], neighbours[k]) for k in range(4)]
    for copy in weight_copies:
        copy.start()
    for copy in weight_copies:
        copy.wait_recv()

    def stack(c, g, out):
        a = firsts[c][2] if g == 0 else firsts[c][0]
        raw_block(c, g, a).wait_recv()

        def tile(n, carry):
            cols = pl.ds(pl.multiple_of(n * 256, 256), 256)
            lhs = jnp.concatenate(
                [xr[c, a].reshape(128, WIDE), r1[c, g].reshape(128, WIDE)], axis=0
            )
            h = jnp.dot(lhs, table[:, cols], preferred_element_type=F32)
            for b in range(4):
                sums = [jnp.zeros((8, 256), F32)] * 3
                for s in range(2):
                    for d in range(4):
                        at = s * 128 + b * 32 + d * 8
                        hh = h[at : at + 8]
                        xx = (xr[c, a, b, d, :, cols] if s == 0 else r1[c, g, b, d, :, cols]).astype(F32)
                        w = ww[0, d] if s == 0 else wn[c, 0, d]
                        q = ww[1, d] if s == 0 else wn[c, 1, d]
                        w = jnp.concatenate([w, w], axis=1)
                        q = jnp.concatenate([q, q], axis=1)
                        inverse = lax.rsqrt(xx * xx + hh * hh + q)
                        sums = [sums[0] + w * xx, sums[1] + xx * inverse, sums[2] + hh * inverse]
                for k in range(3):
                    out[c, b, k, :, cols] = sums[k]
            return carry

        lax.fori_loop(0, 8, tile, 0)

    def second_order(c):
        v, q1, q2, v2 = seconds[c]
        return (v2, q1, q2, v)

    def sums_first(c, k):
        b = second_order(c)[k]
        return remote(s1.at[c, b], r2.at[c, b], b_s.at[c, k], b_r.at[c, k], at_first(c, firsts[c][2]))

    def sums_second(c, k):
        b = second_order(c)[k]
        return remote(s2.at[c, b], r3.at[c, k], c_s.at[c, k], c_r.at[c, k], at_second(c, seconds[c][1]))

    def sums_third(c):
        b = second_order(c)[2]
        return remote(s2.at[c, b], r4.at[c], d_s.at[c], d_r.at[c], at_second(c, seconds[c][2]))

    def stage_three(c):
        for k in range(2):
            b = second_order(c)[k]
            sums_first(c, k).wait_recv()
            s2[c, b] = s2[c, b] + r2[c, b]
            sums_second(c, k).start()

    def stage_four(c):
        b = second_order(c)[2]
        sums_first(c, 2).wait_recv()
        sums_second(c, 0).wait_recv()
        s2[c, b] = s2[c, b] + r2[c, b] + r3[c, 0]
        sums_third(c).start()

    def finish(c):
        b = second_order(c)[3]
        sums_first(c, 3).wait_recv()
        sums_second(c, 1).wait_recv()
        sums_third(c).wait_recv()
        linear, real, imag = [s2[c, b, k] + r2[c, b, k] + r3[c, 1, k] + r4[c, k] for k in range(3)]
        n = counts_ref[pl.ds(8 * c, 8), :]
        n = jnp.concatenate([n] * 16, axis=1)
        linear = linear / n
        lin_ref[pl.ds(8 * c, 8), :] = linear[:, :LAGS]
        pw_ref[pl.ds(8 * c, 8), :] = (linear * ((real * real + imag * imag) / (n * n)))[:, :LAGS]

    for c in range(4):
        stack(c, 0, s1)
        for k in range(4):
            sums_first(c, k).start()
    for c in range(4):
        stack(c, 1, s2)
        if c:
            stage_three(c - 1)
    stage_three(3)
    for c in range(4):
        stage_four(c)
    for c in range(4):
        finish(c)

    for copy in energy_copies + weight_copies:
        copy.wait_send()
    for c in range(4):
        for g in range(2):
            raw_block(c, g, x).wait_send()
        for k in range(4):
            sums_first(c, k).wait_send()
        for k in range(2):
            sums_second(c, k).wait_send()
        sums_third(c).wait_send()


def shards(correlations, mask, counts):
    lag_major = jnp.transpose(correlations, (2, 0, 1))
    divisor = jnp.broadcast_to(jnp.maximum(counts.astype(F32), 1.0)[:, None], (32, 128))
    vmem = pl.BlockSpec(memory_space=pltpu.VMEM)
    dma = pltpu.SemaphoreType.DMA
    return pl.pallas_call(
        kernel,
        out_shape=[jax.ShapeDtypeStruct((32, LAGS), F32)] * 2,
        in_specs=[pl.BlockSpec(memory_space=pl.ANY), vmem, vmem, vmem],
        out_specs=[vmem, vmem],
        scratch_shapes=[
            pltpu.VMEM((4, LAGS, 4, 128), BF),
            pltpu.VMEM((8192, 128), F32),
            pltpu.VMEM((4, 4, 4, 4, 8, WIDE), BF),
            pltpu.VMEM((4, 2, 4, 4, 8, WIDE), BF),
            pltpu.VMEM((WIDE, WIDE), BF),
            pltpu.VMEM((4, 4, 3, 8, WIDE), F32),
            pltpu.VMEM((4, 4, 3, 8, WIDE), F32),
            pltpu.VMEM((4, 4, 3, 8, WIDE), F32),
            pltpu.VMEM((4, 2, 3, 8, WIDE), F32),
            pltpu.VMEM((4, 3, 8, WIDE), F32),
            pltpu.VMEM((8, 2, 8, 128), F32),
            pltpu.VMEM((2, 4, 8, 128), F32),
            pltpu.VMEM((4, 2, 4, 8, 128), F32),
            dma((4,)),
            dma((4, 2)), dma((4, 2)),
            dma((4, 4)), dma((4, 4)),
            dma((4, 2)), dma((4, 2)),
            dma((4,)), dma((4,)),
            dma((8,)), dma((8,)),
            dma((4,)), dma((4,)),
        ],
        compiler_params=pltpu.CompilerParams(
            collective_id=0, has_side_effects=True, vmem_limit_bytes=67043328
        ),
    )(lag_major, mask, divisor, hilbert_rows())


def solution(mesh):
    placed = (P("day", "pair", None), P("day", "pair"), P(("pair", "day")))
    return jax.shard_map(
        shards,
        mesh=mesh,
        in_specs=placed,
        out_specs=(P(("pair", "day"), None), P(("pair", "day"), None)),
        check_vma=False,
    )
```

time: 234 us -> 89.2 us (0.38); the launches traced: 230 us -> 89 us
  other arithmetic: 99.1 us -> 2.02 us
  Pallas kernels: 0 us -> 82.4 us
  waiting for transfers between devices: 56.9 us -> 0 us
  matrix products: 25.2 us -> 0 us
  local copies, waits for them, and re-layouts: 23.2 us -> 4.01 us
  starting transfers between devices: 14.4 us -> 0 us
  blocking collectives: 10.5 us -> 0 us
    reduce_sum x5 -> x0, other arithmetic: 97.3 us -> none  [the longest x1 82.2 us: stack_terms(): jnp.sum(real_part * inverse, axis=0)]
    pallas_call x0 -> x1, Pallas kernels: none -> 82.4 us  [shards(): pl.pallas_call(kernel, out_shape=[jax.ShapeDtypeStruct((32, LAGS), F32)]...]
    all_to_all x2 -> x0, waiting for transfers between devices: 56.9 us -> none  [the longest x1 56.9 us: shards(): lax.all_to_all(blocks, 'day', split_axis=1, concat_axis=0, tiled=True)[:, 0]]
    dot_general x1 -> x0, matrix products: 25.2 us -> none  [stack_terms(): jnp.dot(flattened, kernel_table, preferred_element_type=jnp.float32)]
    all_to_all x2 -> x0, starting transfers between devices: 14.4 us -> none  [the longest x1 7.41 us: shards(): lax.all_to_all(blocks, 'day', split_axis=1, concat_axis=0, tiled=True)[:, 0]]
    all_to_all x1 -> x0, blocking collectives: 10.5 us -> none  [copy_for_each(): lax.all_to_all(jnp.broadcast_to(x[None], (count, *x.shape)), axis, 0, 0,...]
    unnamed x5 -> x2, local copies, waits for them, and re-layouts: 13.8 us -> 3.34 us
    reshape x1 -> x0, local copies, waits for them, and re-layouts: 8.25 us -> none  [shards(): masked.reshape(correlations.shape[0], groups, owned_rows, lag_count)]
  transfers between devices with their start and end apart: 2 -> 0, of which waited for: 1 -> 0; matrix products, arithmetic and copies ran while one was open for 40% -> 0% of each run, Pallas kernels for 0% -> 0%
where the time goes in v1:
time: 89.2 us; the launch traced here: 89 us
  Pallas kernels  82.4 us (92%)
  local copies, waits for them, and re-layouts  4.01 us (4%)
  other arithmetic  2.02 us (2%)
    pallas_call x1, Pallas kernels, shards(): pl.pallas_call(kernel, out_shape=[jax.ShapeDtypeStruct((32, LAGS), F32)]...  82.4 us
    unnamed x2, local copies, waits for them, and re-layouts  3.34 us

profile of v1, /device:TPU:0, one launch (start us, length us, event | category | flops | bytes accessed | tf_op | source)
XLA Modules:
  0.0 89.0 jit_solution(2181946421075256559)
XLA Ops:
  0.6 0.7 convert_maximum_fusion
  1.3 0.7 broadcast_in_dim.11.counts_ref
  2.0 1.4 %fusion.6.rows_ref = f32[8,4096]{1,0:T(8,128)} fusion(s32[4096]{0:T(1024)S(1)} %iota_add_fusion, pred[4096]{0:T(1024)(128)(4,1)S(1)} %iota_compare_fusion), kind=kLoop, calls=%fused_computation.11 | loop fusion | flops 1146880 | bytes 151552 | tf_op jit(solution)/shard_map/jit(_where)/select_n | solution.py:32
  3.3 82.4 %shard_map.50 = (f32[32,2001]{1,0:T(8,128)}, f32[32,2001]{1,0:T(8,128)}) custom-call(bf16[2001,4,512]{2,1,0:T(4,128)(2,1)} %bitcast.1, s32[4,512]{1,0:T(4,128)} %mask_ref.1, f32[32,128]{1,0:T(8,128)} %broadcast_in_dim.11.counts_ref, f32[8,4096]{1,0:T(8,128)} %fusion.6.rows_ref), custom_call_target="tpu_custom_call" | custom-call | tf_op jit(solution)/shard_map/pallas_call | solution.py:269
  85.7 1.7 %copy.7 = f32[32,2001]{1,0:T(8,128)} copy(f32[32,2001]{1,0:T(8,128)} %get-tuple-element.4) | data formatting | bytes 512256
  87.4 1.7 %copy.8 = f32[32,2001]{1,0:T(8,128)} copy(f32[32,2001]{1,0:T(8,128)} %get-tuple-element.5) | data formatting | bytes 512256
  (2 shorter events, 0.0 us)

commit v2 on v1

--- a/solution.py
+++ b/solution.py
@@ -24,16 +24,15 @@
     u = lax.broadcasted_iota(jnp.int32, (8, 4096), 1)
     s = lax.broadcasted_iota(jnp.int32, (8, 4096), 0)
     t = jnp.where(u < 3840, u, u - 4096) - 1792 - s
-    offset = (t + 4 * LAGS) % LAGS
-    offset = jnp.where(offset > LAGS // 2, offset - LAGS, offset)
+    offset = jnp.where(t > LAGS // 2, t - LAGS, jnp.where(t < -(LAGS // 2), t + LAGS, t))
     phase_angle = jnp.pi * offset.astype(F32) / LAGS
-    parity = 1.0 - 2.0 * (offset % 2).astype(F32)
+    parity = 1.0 - 2.0 * (offset & 1).astype(F32)
     sine_safe = jnp.where(offset == 0, 1.0, jnp.sin(phase_angle))
     return jnp.where(offset == 0, 0.0, (jnp.cos(phase_angle) - parity) / (LAGS * sine_safe))
 
 
-def kernel(x_hbm, mask_ref, counts_ref, rows_ref, pw_ref, lin_ref,
-           slab, flat, xr, r1, table, s1, s2, r2, r3, r4, en, ww, wn,
+def kernel(x_hbm, mask_ref, sums_ref,
+           slab, flat, xr, r1, table, s1, s2, coded, r2, r3, r4, en, ww, wn, unit, hil, rows_ref,
            in_sem, a_s, a_r, b_s, b_r, c_s, c_r, d_s, d_r, e_s, e_r, w_s, w_r):
     day = lax.axis_index("day")
     pair = lax.axis_index("pair")
@@ -61,14 +60,14 @@
 
     order = (x2, xa, xb, x)
     loads = [load_block(i, cb) for i, cb in enumerate(order)]
-    for load in loads:
-        load.start()
+    loads[0].start()
 
     barrier = pltpu.get_barrier_semaphore()
     for to in neighbours + peers:
         pl.semaphore_signal(barrier, inc=1, device_id=to, device_id_type=MESH)
 
     flat[pl.ds(8000, 192), :] = jnp.zeros((192, 128), F32)
+    rows_ref[...] = hilbert_rows()
 
     def remote(src, dst, send, recv, to):
         return pltpu.make_async_remote_copy(
@@ -85,6 +84,8 @@
     used = jnp.zeros((8, 128), F32)
     for i, cb in enumerate(order):
         loads[i].wait()
+        if i < 3:
+            loads[i + 1].start()
         cols = pl.ds(pl.multiple_of(cb * 128, 128), 128)
         m4 = mask_ref[:, cols].astype(F32)
         m8 = jnp.concatenate([m4, m4], axis=0)
@@ -119,15 +120,8 @@
             pl.semaphore_wait(barrier, len(neighbours) + len(peers))
             for c in range(2):
                 raw_block(c, 0, x2).start()
-        if i == 1:
-            raw_block(0, 1, xa).start()
-        if i == 2:
-            raw_block(1, 1, xb).start()
         for c in range(2, 4):
             raw_piece(c, 0, y2, cb).start()
-    for c in range(2, 4):
-        for cb in order:
-            raw_piece(c, 1, firsts[c][1], cb).start()
 
     en[0, 0] = squares
     en[0, 1] = used
@@ -155,43 +149,94 @@
     pairs_used = jnp.sum(pairs_used[:4], axis=1, keepdims=True)
     level = energy / (LAGS * jnp.maximum(pairs_used, 1.0)) + 0.1
     weight = lax.rsqrt(level)
+    reach = weight * jnp.sqrt(energy)
     for d in range(4):
         ww[0, d] = jnp.broadcast_to(weight[d : d + 1], (8, 128))
         ww[1, d] = jnp.broadcast_to(0.25 * level[d : d + 1], (8, 128))
+        ww[2, d] = jnp.broadcast_to(reach[d : d + 1], (8, 128))
     weight_copies = [remote(ww, wn.at[k], w_s.at[k], w_r.at[k], neighbours[k]) for k in range(4)]
     for copy in weight_copies:
         copy.start()
-    for copy in weight_copies:
-        copy.wait_recv()
-
-    def stack(c, g, out):
-        a = firsts[c][2] if g == 0 else firsts[c][0]
-        raw_block(c, g, a).wait_recv()
-
-        def tile(n, carry):
+    for c in range(4):
+        raw_block(c, 1, firsts[c][1]).start()
+
+    def scale_up(c):
+        reach = jnp.maximum(jnp.max(ww[2], axis=0), jnp.max(wn[c, 2], axis=0))
+        units = jnp.stack([reach, jnp.minimum(1.0, 2.0 * reach)]) * 2.0**-12.5
+        unit[c] = jnp.maximum(units, 1e-30).astype(BF).astype(F32)
+
+    def code(v, u):
+        t = v * (1.0 / u)
+        t = t * t
+        t = t * t
+        t = t * t
+        return jnp.where(v < 0.0, -t, t)
+
+    def decode(ref):
+        y = ref[...].astype(F32)
+        size = jnp.exp(0.125 * jnp.log(jnp.abs(y))) * y_unit(ref)
+        return jnp.where(y < 0.0, -size, size)
+
+    def y_unit(ref):
+        return ref[:, :, WIDE - 1 : WIDE].astype(F32)
+
+    def stack(cs, g, far):
+        own = [firsts[c][2] if g == 0 else firsts[c][0] for c in cs]
+        out = s2 if g else s1
+        if far:
+            for c in cs:
+                raw_block(c, g, x).wait_recv()
+
+        def rows_of(i):
+            c = cs[i]
+            return r1.at[c, g] if far else xr.at[c, own[i]]
+
+        def matmul(n, slot):
             cols = pl.ds(pl.multiple_of(n * 256, 256), 256)
-            lhs = jnp.concatenate(
-                [xr[c, a].reshape(128, WIDE), r1[c, g].reshape(128, WIDE)], axis=0
-            )
-            h = jnp.dot(lhs, table[:, cols], preferred_element_type=F32)
-            for b in range(4):
-                sums = [jnp.zeros((8, 256), F32)] * 3
-                for s in range(2):
-                    for d in range(4):
-                        at = s * 128 + b * 32 + d * 8
-                        hh = h[at : at + 8]
-                        xx = (xr[c, a, b, d, :, cols] if s == 0 else r1[c, g, b, d, :, cols]).astype(F32)
-                        w = ww[0, d] if s == 0 else wn[c, 0, d]
-                        q = ww[1, d] if s == 0 else wn[c, 1, d]
-                        w = jnp.concatenate([w, w], axis=1)
-                        q = jnp.concatenate([q, q], axis=1)
-                        inverse = lax.rsqrt(xx * xx + hh * hh + q)
-                        sums = [sums[0] + w * xx, sums[1] + xx * inverse, sums[2] + hh * inverse]
-                for k in range(3):
-                    out[c, b, k, :, cols] = sums[k]
+            lhs = jnp.concatenate([rows_of(i)[...].reshape(128, WIDE) for i in range(2)], axis=0)
+            hil[slot] = jnp.dot(lhs, table[:, cols], preferred_element_type=F32)
+
+        def combine(n, slot):
+            for i, c in enumerate(cs):
+                for half in range(2):
+                    cols = pl.ds(pl.multiple_of(n * 256 + half * 128, 128), 128)
+                    for b in range(4):
+                        if far:
+                            sums = [out[c, b, k, :, cols] for k in range(3)]
+                        else:
+                            sums = [jnp.zeros((8, 128), F32)] * 3
+                        for d in range(4):
+                            at = i * 128 + b * 32 + d * 8
+                            hh = hil[slot, at : at + 8, half * 128 : half * 128 + 128]
+                            xx = rows_of(i)[b, d, :, cols].astype(F32)
+                            w = wn[c, 0, d] if far else ww[0, d]
+                            q = wn[c, 1, d] if far else ww[1, d]
+                            inverse = lax.rsqrt(xx * xx + hh * hh + q)
+                            sums = [sums[0] + w * xx, sums[1] + xx * inverse, sums[2] + hh * inverse]
+                        for k in range(3):
+                            if far and g == 0:
+                                u = unit[c, min(k, 1)]
+                                y = code(sums[k], u)
+                                if isinstance(n, int) and n == 7 and half == 1:
+                                    lane = lax.broadcasted_iota(jnp.int32, (8, 128), 1)
+                                    y = jnp.where(lane == 127, u, y)
+                                coded[c, b, k, :, cols] = y.astype(BF)
+                            else:
+                                out[c, b, k, :, cols] = sums[k]
+
+        matmul(0, 0)
+
+        def tiles(m, carry):
+            matmul(2 * m + 1, 1)
+            combine(2 * m, 0)
+            matmul(2 * m + 2, 0)
+            combine(2 * m + 1, 1)
             return carry
 
-        lax.fori_loop(0, 8, tile, 0)
+        lax.fori_loop(0, 3, tiles, 0)
+        matmul(7, 1)
+        combine(6, 0)
+        combine(7, 1)
 
     def second_order(c):
         v, q1, q2, v2 = seconds[c]
@@ -199,7 +244,7 @@
 
     def sums_first(c, k):
         b = second_order(c)[k]
-        return remote(s1.at[c, b], r2.at[c, b], b_s.at[c, k], b_r.at[c, k], at_first(c, firsts[c][2]))
+        return remote(coded.at[c, b], r2.at[c, b], b_s.at[c, k], b_r.at[c, k], at_first(c, firsts[c][2]))
 
     def sums_second(c, k):
         b = second_order(c)[k]
@@ -213,14 +258,14 @@
         for k in range(2):
             b = second_order(c)[k]
             sums_first(c, k).wait_recv()
-            s2[c, b] = s2[c, b] + r2[c, b]
+            s2[c, b] = s2[c, b] + decode(r2.at[c, b])
             sums_second(c, k).start()
 
     def stage_four(c):
         b = second_order(c)[2]
         sums_first(c, 2).wait_recv()
         sums_second(c, 0).wait_recv()
-        s2[c, b] = s2[c, b] + r2[c, b] + r3[c, 0]
+        s2[c, b] = s2[c, b] + decode(r2.at[c, b]) + r3[c, 0]
         sums_third(c).start()
 
     def finish(c):
@@ -228,22 +273,25 @@
         sums_first(c, 3).wait_recv()
         sums_second(c, 1).wait_recv()
         sums_third(c).wait_recv()
-        linear, real, imag = [s2[c, b, k] + r2[c, b, k] + r3[c, 1, k] + r4[c, k] for k in range(3)]
-        n = counts_ref[pl.ds(8 * c, 8), :]
-        n = jnp.concatenate([n] * 16, axis=1)
-        linear = linear / n
-        lin_ref[pl.ds(8 * c, 8), :] = linear[:, :LAGS]
-        pw_ref[pl.ds(8 * c, 8), :] = (linear * ((real * real + imag * imag) / (n * n)))[:, :LAGS]
-
-    for c in range(4):
-        stack(c, 0, s1)
-        for k in range(4):
-            sums_first(c, k).start()
-    for c in range(4):
-        stack(c, 1, s2)
-        if c:
-            stage_three(c - 1)
-    stage_three(3)
+        total = s2[c, b] + decode(r2.at[c, b]) + r3[c, 1] + r4[c]
+        sums_ref[:, pl.ds(8 * c, 8), :] = total[:, :, :LAGS]
+
+    stack((0, 1), 0, False)
+    stack((2, 3), 0, False)
+    for copy in weight_copies:
+        copy.wait_recv()
+    for c in range(4):
+        scale_up(c)
+    for cs in ((0, 1), (2, 3)):
+        stack(cs, 0, True)
+        for c in cs:
+            for k in range(4):
+                sums_first(c, k).start()
+    for cs in ((0, 1), (2, 3)):
+        stack(cs, 1, False)
+        stack(cs, 1, True)
+        for c in cs:
+            stage_three(c)
     for c in range(4):
         stage_four(c)
     for c in range(4):
@@ -263,14 +311,13 @@
 
 def shards(correlations, mask, counts):
     lag_major = jnp.transpose(correlations, (2, 0, 1))
-    divisor = jnp.broadcast_to(jnp.maximum(counts.astype(F32), 1.0)[:, None], (32, 128))
     vmem = pl.BlockSpec(memory_space=pltpu.VMEM)
     dma = pltpu.SemaphoreType.DMA
-    return pl.pallas_call(
+    linear_sum, phase_real, phase_imag = pl.pallas_call(
         kernel,
-        out_shape=[jax.ShapeDtypeStruct((32, LAGS), F32)] * 2,
-        in_specs=[pl.BlockSpec(memory_space=pl.ANY), vmem, vmem, vmem],
-        out_specs=[vmem, vmem],
+        out_shape=jax.ShapeDtypeStruct((3, 32, LAGS), F32),
+        in_specs=[pl.BlockSpec(memory_space=pl.ANY), vmem],
+        out_specs=vmem,
         scratch_shapes=[
             pltpu.VMEM((4, LAGS, 4, 128), BF),
             pltpu.VMEM((8192, 128), F32),
@@ -279,12 +326,16 @@
             pltpu.VMEM((WIDE, WIDE), BF),
             pltpu.VMEM((4, 4, 3, 8, WIDE), F32),
             pltpu.VMEM((4, 4, 3, 8, WIDE), F32),
-            pltpu.VMEM((4, 4, 3, 8, WIDE), F32),
+            pltpu.VMEM((4, 4, 3, 8, WIDE), BF),
+            pltpu.VMEM((4, 4, 3, 8, WIDE), BF),
             pltpu.VMEM((4, 2, 3, 8, WIDE), F32),
             pltpu.VMEM((4, 3, 8, WIDE), F32),
             pltpu.VMEM((8, 2, 8, 128), F32),
-            pltpu.VMEM((2, 4, 8, 128), F32),
-            pltpu.VMEM((4, 2, 4, 8, 128), F32),
+            pltpu.VMEM((3, 4, 8, 128), F32),
+            pltpu.VMEM((4, 3, 4, 8, 128), F32),
+            pltpu.VMEM((4, 2, 8, 128), F32),
+            pltpu.VMEM((2, 256, 256), F32),
+            pltpu.VMEM((8, 4096), F32),
             dma((4,)),
             dma((4, 2)), dma((4, 2)),
             dma((4, 4)), dma((4, 4)),
@@ -296,7 +347,11 @@
         compiler_params=pltpu.CompilerParams(
             collective_id=0, has_side_effects=True, vmem_limit_bytes=67043328
         ),
-    )(lag_major, mask, divisor, hilbert_rows())
+    )(lag_major, mask)
+    divisor = jnp.maximum(counts.astype(F32), 1.0)[:, None]
+    linear = linear_sum / divisor
+    coherence = (phase_real * phase_real + phase_imag * phase_imag) / (divisor * divisor)
+    return (linear * coherence, linear)
 
 
 def solution(mesh):

time: 89.2 us -> 74.8 us (0.84)
  Pallas kernels: 82.4 us -> 70.3 us
  local copies, waits for them, and re-layouts: 4.01 us -> 0 us
  other arithmetic: 2.02 us -> 3.22 us
    pallas_call x1, Pallas kernels: 82.4 us -> 70.3 us  [shards(): pl.pallas_call(kernel, out_shape=jax.ShapeDtypeStruct((3, 32, LAGS), F32)...]
    unnamed x2 -> x0, local copies, waits for them, and re-layouts: 3.34 us -> none
    mul x0 -> x1, other arithmetic: none -> 2.02 us  [shards(): return (linear * coherence, linear)]
    select_n x1 -> x0, other arithmetic: 1.35 us -> none  [hilbert_rows(): jnp.where(offset == 0, 0.0, (jnp.cos(phase_angle) - parity) / (LAGS * sin...]
where the time goes in v2:
time: 74.8 us; the launch traced here: 74.1 us
  Pallas kernels  70.3 us (94%)
  other arithmetic  3.22 us (4%)
    pallas_call x1, Pallas kernels, shards(): pl.pallas_call(kernel, out_shape=jax.ShapeDtypeStruct((3, 32, LAGS), F32)...  70.3 us
    mul x1, other arithmetic, shards(): return (linear * coherence, linear)  2.02 us

profile of v2, /device:TPU:0, one launch (start us, length us, event | category | flops | bytes accessed | tf_op | source)
XLA Modules:
  0.0 74.1 jit_solution(1709242809187585630)
XLA Ops:
  0.6 1.2 %convert_maximum_fusion = (f32[32]{0:T(128)}, f32[32]{0:T(128)}) fusion(s32[32]{0:T(128)} %param.5), kind=kLoop, calls=%fused_computation.3 | loop fusion | flops 96 | bytes 384 | tf_op jit(solution)/shard_map/max | solution.py:351
  1.8 70.3 %shard_map.50 = f32[3,32,2001]{2,1,0:T(8,128)} custom-call(bf16[2001,4,512]{2,1,0:T(4,128)(2,1)} %bitcast.8, s32[4,512]{1,0:T(4,128)} %mask_ref.1), custom_call_target="tpu_custom_call" | custom-call | tf_op jit(solution)/shard_map/pallas_call | solution.py:316
  72.1 2.0 %fusion = (f32[32,2001]{1,0:T(8,128)}, f32[32,2001]{1,0:T(8,128)}) fusion(f32[3,32,2001]{2,1,0:T(8,128)} %shard_map.50, f32[32]{0:T(128)} %get-tuple-element.5, f32[32]{0:T(128)} %get-tuple-element.4), kind=kLoop, calls=%fused_computation.1 | loop fusion | flops 384192 | bytes 1280896 | tf_op jit(solution)/shard_map/mul | solution.py:354

commit v3 on v2

v3 whole, which is shorter than its diff:
```python
import jax
import jax.numpy as jnp
from jax import lax
from jax.experimental import pallas as pl
from jax.experimental.pallas import tpu as pltpu
from jax.sharding import PartitionSpec as P

BF = jnp.bfloat16
F32 = jnp.float32
MESH = pl.DeviceIdType.MESH
LAGS = 2001
WIDE = 2048


def alpha(v):
    return v + 1 - 2 * (v % 2)


def beta(v):
    return 3 - v


def hilbert_rows():
    u = lax.broadcasted_iota(jnp.int32, (8, 4096), 1)
    s = lax.broadcasted_iota(jnp.int32, (8, 4096), 0)
    t = jnp.where(u < 3840, u, u - 4096) - 1792 - s
    offset = jnp.where(t > LAGS // 2, t - LAGS, jnp.where(t < -(LAGS // 2), t + LAGS, t))
    phase_angle = jnp.pi * offset.astype(F32) / LAGS
    parity = 1.0 - 2.0 * (offset & 1).astype(F32)
    sine_safe = jnp.where(offset == 0, 1.0, jnp.sin(phase_angle))
    return jnp.where(offset == 0, 0.0, (jnp.cos(phase_angle) - parity) / (LAGS * sine_safe))


def kernel(x_hbm, mask_ref, counts_ref, sums_ref,
           slab, flat, xr, r1, table, s1, s2, coded, r2, r3, r4, en, ww, wn, unit, hil, rows_ref,
           in_sem, a_s, a_r, b_s, b_r, c_s, c_r, d_s, d_r, e_s, e_r, w_s, w_r):
    day = lax.axis_index("day")
    pair = lax.axis_index("pair")
    x = day // 4
    y = day % 4
    xa, xb, ya, yb = alpha(x), beta(x), alpha(y), beta(y)
    x2, y2 = (x + 2) % 4, (y + 2) % 4
    along_x_a, along_x_b = (x, xa, xb, x2), (x, xb, xa, x2)
    along_y_a, along_y_b = (y, ya, yb, y2), (y, yb, ya, y2)
    firsts = (along_x_a, along_x_b, along_y_a, along_y_b)
    seconds = (along_y_a, along_y_b, along_x_a, along_x_b)

    def at_first(c, v):
        return (v * 4 + y, pair) if c < 2 else (x * 4 + v, pair)

    def at_second(c, v):
        return (x * 4 + v, pair) if c < 2 else (v * 4 + y, pair)

    neighbours = [(xa * 4 + y, pair), (xb * 4 + y, pair), (x * 4 + ya, pair), (x * 4 + yb, pair)]
    peers = [(day, (pair + k) % 8) for k in range(1, 8)]

    def load_block(i, cb):
        cols = pl.ds(pl.multiple_of(cb * 128, 128), 128)
        return pltpu.make_async_copy(x_hbm.at[:, :, cols], slab.at[i], in_sem.at[i])

    order = (x2, xa, xb, x)
    loads = [load_block(i, cb) for i, cb in enumerate(order)]
    loads[0].start()

    barrier = pltpu.get_barrier_semaphore()
    for to in neighbours + peers:
        pl.semaphore_signal(barrier, inc=1, device_id=to, device_id_type=MESH)

    for i in range(3):
        flat[i, pl.ds(8000, 192), :] = jnp.zeros((192, 128), F32)
    rows_ref[...] = hilbert_rows()

    def remote(src, dst, send, recv, to):
        return pltpu.make_async_remote_copy(
            src_ref=src, dst_ref=dst, send_sem=send, recv_sem=recv, device_id=to, device_id_type=MESH
        )

    def raw_block(c, g, a):
        return remote(xr.at[c, a], r1.at[c, g], a_s.at[c, g], a_r.at[c, g], at_first(c, firsts[c][1]))

    def raw_piece(c, g, a, b):
        return remote(xr.at[c, a, b], r1.at[c, g, b], a_s.at[c, g], a_r.at[c, g], at_first(c, firsts[c][1]))

    totals = [jnp.zeros((8, 128), F32), jnp.zeros((8, 128), F32)]

    def widen(i):
        loads[i].wait()
        if i < 3:
            loads[i + 1].start()
        cols = pl.ds(pl.multiple_of(order[i] * 128, 128), 128)
        m4 = mask_ref[:, cols].astype(F32)
        m8 = jnp.concatenate([m4, m4], axis=0)
        rows = slab.at[i].reshape(4 * LAGS, 128)
        into = flat.at[max(i - 1, 0)]

        def step(j, acc):
            at = pl.ds(pl.multiple_of(j * 32, 32), 32)
            v = rows[at, :].astype(F32).reshape(4, 8, 128) * m8[None]
            into[at, :] = v.reshape(32, 128)
            return acc + jnp.sum(v * v, axis=0)

        squares = lax.fori_loop(0, 250, step, totals[0], unroll=10)
        last = rows[pl.ds(8000, 4), :].astype(F32) * m4
        into[pl.ds(8000, 4), :] = last
        totals[0] = squares + jnp.concatenate([last * last, jnp.zeros((4, 128), F32)], axis=0)
        totals[1] = totals[1] + m8

    def turn(i):
        cb = order[i]
        source = flat.at[max(i - 1, 0)]

        def step(j, carry):
            lags = pl.ds(pl.multiple_of(j * 128, 128), 128)
            for d in range(4):
                t = source[pl.ds(pl.multiple_of(j * 512, 512) + d, 128, stride=4), :]
                t = t.astype(BF).T.reshape(4, 4, 8, 128)
                for c in range(2):
                    xr[c, cb, :, d, :, lags] = t[:, c]
                for c in range(2, 4):
                    for q in range(4):
                        xr[c, q, cb, d, :, lags] = t[q, c]
            return carry

        lax.fori_loop(0, 16, step, 0, unroll=2)
        if i == 0:
            pl.semaphore_wait(barrier, len(neighbours) + len(peers))
            for c in range(2):
                raw_block(c, 0, x2).start()
        for c in range(2, 4):
            raw_piece(c, 0, y2, cb).start()

    widen(0)
    turn(0)
    widen(1)
    widen(2)
    widen(3)

    en[0, 0] = totals[0]
    en[0, 1] = totals[1]
    energy_copies = [
        remote(en.at[0], en.at[k], e_s.at[k], e_r.at[k], peers[k - 1]) for k in range(1, 8)
    ]
    for copy in energy_copies:
        copy.start()
    turn(1)
    turn(2)
    turn(3)

    def tabulate(j, carry):
        lo = pltpu.roll(rows_ref[...], j * 16, 1)
        hi = pltpu.roll(rows_ref[...], j * 16 + 8, 1)
        both = jnp.concatenate([lo, hi], axis=0).astype(BF)
        for a in range(8):
            table[pl.ds(pl.multiple_of(a * 256 + j * 16, 16), 16), :] = both[:, 256 * (7 - a) : 256 * (7 - a) + WIDE]
        return carry

    lax.fori_loop(0, 16, tabulate, 0)

    for copy in energy_copies:
        copy.wait_recv()
    total = jnp.sum(en[:, 0], axis=0)
    pairs_used = jnp.sum(en[:, 1], axis=0)
    energy = jnp.sum(total[:4] + total[4:], axis=1, keepdims=True)
    pairs_used = jnp.sum(pairs_used[:4], axis=1, keepdims=True)
    level = energy / (LAGS * jnp.maximum(pairs_used, 1.0)) + 0.1
    weight = lax.rsqrt(level)
    reach = weight * jnp.sqrt(energy)
    for d in range(4):
        ww[0, d] = jnp.broadcast_to(weight[d : d + 1], (8, 128))
        ww[1, d] = jnp.broadcast_to(0.25 * level[d : d + 1], (8, 128))
        ww[2, d] = jnp.broadcast_to(reach[d : d + 1], (8, 128))
    weight_copies = [remote(ww, wn.at[k], w_s.at[k], w_r.at[k], neighbours[k]) for k in range(4)]
    for copy in weight_copies:
        copy.start()
    for c in range(4):
        raw_block(c, 1, firsts[c][1]).start()

    def scale_up(c):
        reach = jnp.maximum(jnp.max(ww[2], axis=0), jnp.max(wn[c, 2], axis=0))
        units = jnp.stack([reach, jnp.minimum(1.0, 2.0 * reach)]) * 2.0**-12.5
        unit[c] = jnp.maximum(units, 1e-30).astype(BF).astype(F32)

    def code(v, u):
        t = v * (1.0 / u)
        t = t * t
        t = t * t
        t = t * t
        return jnp.where(v < 0.0, -t, t)

    def decode(ref):
        y = ref[...].astype(F32)
        size = jnp.exp(0.125 * jnp.log(jnp.abs(y))) * y_unit(ref)
        return jnp.where(y < 0.0, -size, size)

    def y_unit(ref):
        return ref[:, :, WIDE - 1 : WIDE].astype(F32)

    def second_order(c):
        v, q1, q2, v2 = seconds[c]
        return (v2, q1, q2, v)

    def tile_sums(parts, slot, half, cols, sums):
        for at, raw, wq in parts:
            for d in range(4):
                hh = hil[slot, at + 8 * d : at + 8 * d + 8, half * 128 : half * 128 + 128]
                xx = raw[d, :, cols].astype(F32)
                inverse = lax.rsqrt(xx * xx + hh * hh + wq[1, d])
                sums = [sums[0] + wq[0, d] * xx, sums[1] + xx * inverse, sums[2] + hh * inverse]
        return sums

    def halves(n):
        for half in range(2):
            yield half, pl.ds(pl.multiple_of(n * 256 + half * 128, 128), 128)

    class FirstSums:
        def __init__(self, cs, far):
            self.cs, self.far = cs, far

        def before(self):
            if self.far:
                if self.cs[0] == 0:
                    for copy in weight_copies:
                        copy.wait_recv()
                    for c in range(4):
                        scale_up(c)
                for c in self.cs:
                    raw_block(c, 0, x).wait_recv()

        def rows(self, c):
            return r1.at[c, 0] if self.far else xr.at[c, firsts[c][2]]

        def left(self):
            return [self.rows(c)[...].reshape(128, WIDE) for c in self.cs]

        def combine(self, n, slot):
            for i, c in enumerate(self.cs):
                wq = wn.at[c] if self.far else ww
                for half, cols in halves(n):
                    for b in range(4):
                        sums = [s1[c, b, k, :, cols] for k in range(3)] if self.far else [jnp.zeros((8, 128), F32)] * 3
                        sums = tile_sums([(i * 128 + b * 32, self.rows(c).at[b], wq)], slot, half, cols, sums)
                        for k in range(3):
                            if not self.far:
                                s1[c, b, k, :, cols] = sums[k]
                                continue
                            u = unit[c, min(k, 1)]
                            y = code(sums[k], u)
                            if isinstance(n, int) and n == 7 and half == 1:
                                lane = lax.broadcasted_iota(jnp.int32, (8, 128), 1)
                                y = jnp.where(lane == 127, u, y)
                            coded[c, b, k, :, cols] = y.astype(BF)

        def after(self):
            if self.far:
                for c in self.cs:
                    for k in range(4):
                        sums_first(c, k).start()

    class SecondSums:
        def __init__(self, k):
            self.k = k

        def before(self):
            if self.k == 0:
                for c in range(4):
                    raw_block(c, 1, x).wait_recv()

        def rows(self, c):
            b = second_order(c)[self.k]
            return xr.at[c, firsts[c][0], b], r1.at[c, 1, b]

        def left(self):
            return [r[...].reshape(32, WIDE) for c in range(4) for r in self.rows(c)]

        def combine(self, n, slot):
            for c in range(4):
                own, far = self.rows(c)
                for half, cols in halves(n):
                    parts = [(c * 64, own, ww), (c * 64 + 32, far, wn.at[c])]
                    sums = tile_sums(parts, slot, half, cols, [jnp.zeros((8, 128), F32)] * 3)
                    for k in range(3):
                        s2[c, self.k, k, :, cols] = sums[k]

        def after(self):
            for c in range(4):
                (stage_three, stage_three, stage_four, finish)[self.k](c, self.k)

    def matmul(job, n, slot):
        cols = pl.ds(pl.multiple_of(n * 256, 256), 256)
        lhs = jnp.concatenate(job.left(), axis=0)
        hil[slot] = jnp.dot(lhs, table[:, cols], preferred_element_type=F32)

    def sums_first(c, k):
        b = second_order(c)[k]
        return remote(coded.at[c, b], r2.at[c, k], b_s.at[c, k], b_r.at[c, k], at_first(c, firsts[c][2]))

    def sums_second(c, k):
        return remote(s2.at[c, k], r3.at[c, k], c_s.at[c, k], c_r.at[c, k], at_second(c, seconds[c][1]))

    def sums_third(c):
        return remote(s2.at[c, 2], r4.at[c], d_s.at[c], d_r.at[c], at_second(c, seconds[c][2]))

    def stage_three(c, k):
        sums_first(c, k).wait_recv()
        s2[c, k] = s2[c, k] + decode(r2.at[c, k])
        sums_second(c, k).start()

    def stage_four(c, k):
        sums_first(c, 2).wait_recv()
        sums_second(c, 0).wait_recv()
        s2[c, 2] = s2[c, 2] + decode(r2.at[c, 2]) + r3[c, 0]
        sums_third(c).start()

    def finish(c, k):
        sums_first(c, 3).wait_recv()
        sums_second(c, 1).wait_recv()
        sums_third(c).wait_recv()
        total = s2[c, 3] + decode(r2.at[c, 3]) + r3[c, 1] + r4[c]
        n = counts_column[8 * c : 8 * c + 8]
        sums_ref[0, pl.ds(8 * c, 8), :] = (total[0] / n)[:, :LAGS]
        sums_ref[1, pl.ds(8 * c, 8), :] = ((total[1] * total[1] + total[2] * total[2]) / (n * n))[:, :LAGS]

    counts = jnp.broadcast_to(jnp.maximum(counts_ref[...].astype(F32), 1.0), (32, 32))
    across = lax.broadcasted_iota(jnp.int32, (32, 32), 0) == lax.broadcasted_iota(jnp.int32, (32, 32), 1)
    counts_column = jnp.sum(jnp.where(across, counts, 0.0), axis=1, keepdims=True)

    jobs = [FirstSums(cs, far) for far in (False, True) for cs in ((0, 1), (2, 3))]
    jobs += [SecondSums(k) for k in range(4)]
    matmul(jobs[0], 0, 0)
    for job, following in zip(jobs, jobs[1:] + [None]):

        def tiles(m, carry, job=job):
            matmul(job, 2 * m + 1, 1)
            job.combine(2 * m, 0)
            matmul(job, 2 * m + 2, 0)
            job.combine(2 * m + 1, 1)
            return carry

        lax.fori_loop(0, 3, tiles, 0)
        if following:
            following.before()
        matmul(job, 7, 1)
        job.combine(6, 0)
        if following:
            matmul(following, 0, 0)
        job.combine(7, 1)
        job.after()

    for copy in energy_copies + weight_copies:
        copy.wait_send()
    for c in range(4):
        for g in range(2):
            raw_block(c, g, x).wait_send()
        for k in range(4):
            sums_first(c, k).wait_send()
        for k in range(2):
            sums_second(c, k).wait_send()
        sums_third(c).wait_send()


def shards(correlations, mask, counts):
    lag_major = jnp.transpose(correlations, (2, 0, 1))
    vmem = pl.BlockSpec(memory_space=pltpu.VMEM)
    dma = pltpu.SemaphoreType.DMA
    linear, coherence = pl.pallas_call(
        kernel,
        out_shape=jax.ShapeDtypeStruct((2, 32, LAGS), F32),
        in_specs=[pl.BlockSpec(memory_space=pl.ANY), vmem, vmem],
        out_specs=vmem,
        scratch_shapes=[
            pltpu.VMEM((4, LAGS, 4, 128), BF),
            pltpu.VMEM((3, 8192, 128), F32),
            pltpu.VMEM((4, 4, 4, 4, 8, WIDE), BF),
            pltpu.VMEM((4, 2, 4, 4, 8, WIDE), BF),
            pltpu.VMEM((WIDE, WIDE), BF),
            pltpu.VMEM((4, 4, 3, 8, WIDE), F32),
            pltpu.VMEM((4, 4, 3, 8, WIDE), F32),
            pltpu.VMEM((4, 4, 3, 8, WIDE), BF),
            pltpu.VMEM((4, 4, 3, 8, WIDE), BF),
            pltpu.VMEM((4, 2, 3, 8, WIDE), F32),
            pltpu.VMEM((4, 3, 8, WIDE), F32),
            pltpu.VMEM((8, 2, 8, 128), F32),
            pltpu.VMEM((3, 4, 8, 128), F32),
            pltpu.VMEM((4, 3, 4, 8, 128), F32),
            pltpu.VMEM((4, 2, 8, 128), F32),
            pltpu.VMEM((2, 256, 256), F32),
            pltpu.VMEM((8, 4096), F32),
            dma((4,)),
            dma((4, 2)), dma((4, 2)),
            dma((4, 4)), dma((4, 4)),
            dma((4, 2)), dma((4, 2)),
            dma((4,)), dma((4,)),
            dma((8,)), dma((8,)),
            dma((4,)), dma((4,)),
        ],
        compiler_params=pltpu.CompilerParams(
            collective_id=0, has_side_effects=True, vmem_limit_bytes=58 * 2**20
        ),
    )(lag_major, mask, counts[None])
    return (linear * coherence, linear)


def solution(mesh):
    placed = (P("day", "pair", None), P("day", "pair"), P(("pair", "day")))
    return jax.shard_map(
        shards,
        mesh=mesh,
        in_specs=placed,
        out_specs=(P(("pair", "day"), None), P(("pair", "day"), None)),
        check_vma=False,
    )
```

time: 74.8 us -> 63.5 us (0.85)
  Pallas kernels: 70.3 us -> 60.8 us
  other arithmetic: 3.22 us -> 1.85 us
    pallas_call x1, Pallas kernels: 70.3 us -> 60.8 us  [shards(): pl.pallas_call(kernel, out_shape=jax.ShapeDtypeStruct((2, 32, LAGS), F32)...]
    max x1 -> x0, other arithmetic: 1.2 us -> none  [shards(): divisor = jnp.maximum(counts.astype(F32), 1.0)[:, None]]
where the time goes in v3:
time: 63.5 us; the launch traced here: 63.3 us
  Pallas kernels  60.8 us (96%)
  other arithmetic  1.85 us (3%)
  between operations  0.64 us (1%)
    pallas_call x1, Pallas kernels, shards(): pl.pallas_call(kernel, out_shape=jax.ShapeDtypeStruct((2, 32, LAGS), F32)...  60.8 us
    mul x1, other arithmetic, shards(): return (linear * coherence, linear)  1.85 us

profile of v3, /device:TPU:0, one launch (start us, length us, event | category | flops | bytes accessed | tf_op | source)
XLA Modules:
  0.0 63.3 jit_solution(12847346769258422500)
XLA Ops:
  0.6 60.8 %shard_map.50 = f32[2,32,2001]{2,1,0:T(8,128)} custom-call(bf16[2001,4,512]{2,1,0:T(4,128)(2,1)} %bitcast.7, s32[4,512]{1,0:T(4,128)} %mask_ref.1, s32[1,32]{1,0:T(1,128)} %bitcast.8), custom_call_target="tpu_custom_call" | custom-call | tf_op jit(solution)/shard_map/pallas_call | solution.py:365
  61.4 1.9 %bitcast_multiply_fusion = (f32[32,2001]{1,0:T(8,128)}, f32[32,2001]{1,0:T(8,128)}) fusion(f32[2,32,2001]{2,1,0:T(8,128)} %shard_map.50), kind=kLoop, calls=%fused_computation | loop fusion | flops 64032 | bytes 1024512 | tf_op jit(solution)/shard_map/mul | solution.py:400

commit v4 on v3

--- a/solution.py
+++ b/solution.py
@@ -10,6 +10,7 @@
 MESH = pl.DeviceIdType.MESH
 LAGS = 2001
 WIDE = 2048
+EARLY = 3
 
 
 def alpha(v):
@@ -32,8 +33,8 @@
 
 
 def kernel(x_hbm, mask_ref, counts_ref, sums_ref,
-           slab, flat, xr, r1, table, s1, s2, coded, r2, r3, r4, en, ww, wn, unit, hil, rows_ref,
-           in_sem, a_s, a_r, b_s, b_r, c_s, c_r, d_s, d_r, e_s, e_r, w_s, w_r):
+           slab, flat, xr, r1, table, s1, s2, coded, r2, third, r3, r4, en, ww, wn, unit, hil, rows_ref,
+           in_sem, a_s, a_r, g_s, g_r, b_s, b_r, c_s, c_r, d_s, d_r, e_s, e_r, w_s, w_r):
     day = lax.axis_index("day")
     pair = lax.axis_index("pair")
     x = day // 4
@@ -54,20 +55,23 @@
     neighbours = [(xa * 4 + y, pair), (xb * 4 + y, pair), (x * 4 + ya, pair), (x * 4 + yb, pair)]
     peers = [(day, (pair + k) % 8) for k in range(1, 8)]
 
-    def load_block(i, cb):
-        cols = pl.ds(pl.multiple_of(cb * 128, 128), 128)
-        return pltpu.make_async_copy(x_hbm.at[:, :, cols], slab.at[i], in_sem.at[i])
+    def load(i, start, size, sem):
+        cols = pl.ds(pl.multiple_of(order[i] * 128, 128), 128)
+        lags = pl.ds(start, size)
+        return pltpu.make_async_copy(x_hbm.at[lags, :, cols], slab.at[i % 2, lags], in_sem.at[sem])
 
     order = (x2, xa, xb, x)
-    loads = [load_block(i, cb) for i, cb in enumerate(order)]
-    loads[0].start()
+    first_loads = [load(0, 512 * q, min(512, LAGS - 512 * q), q) for q in range(4)]
+    loads = [None] + [load(i, 0, LAGS, 3 + i) for i in range(1, 4)]
+    for copy in first_loads + [loads[1]]:
+        copy.start()
 
     barrier = pltpu.get_barrier_semaphore()
     for to in neighbours + peers:
         pl.semaphore_signal(barrier, inc=1, device_id=to, device_id_type=MESH)
 
-    for i in range(3):
-        flat[i, pl.ds(8000, 192), :] = jnp.zeros((192, 128), F32)
+    for i in range(2):
+        slab[i, pl.ds(LAGS, WIDE - LAGS)] = jnp.zeros((WIDE - LAGS, 4, 128), BF)
     rows_ref[...] = hilbert_rows()
 
     def remote(src, dst, send, recv, to):
@@ -75,76 +79,54 @@
             src_ref=src, dst_ref=dst, send_sem=send, recv_sem=recv, device_id=to, device_id_type=MESH
         )
 
-    def raw_block(c, g, a):
-        return remote(xr.at[c, a], r1.at[c, g], a_s.at[c, g], a_r.at[c, g], at_first(c, firsts[c][1]))
-
-    def raw_piece(c, g, a, b):
-        return remote(xr.at[c, a, b], r1.at[c, g, b], a_s.at[c, g], a_r.at[c, g], at_first(c, firsts[c][1]))
-
-    totals = [jnp.zeros((8, 128), F32), jnp.zeros((8, 128), F32)]
-
-    def widen(i):
-        loads[i].wait()
-        if i < 3:
-            loads[i + 1].start()
-        cols = pl.ds(pl.multiple_of(order[i] * 128, 128), 128)
-        m4 = mask_ref[:, cols].astype(F32)
-        m8 = jnp.concatenate([m4, m4], axis=0)
-        rows = slab.at[i].reshape(4 * LAGS, 128)
-        into = flat.at[max(i - 1, 0)]
-
-        def step(j, acc):
-            at = pl.ds(pl.multiple_of(j * 32, 32), 32)
-            v = rows[at, :].astype(F32).reshape(4, 8, 128) * m8[None]
-            into[at, :] = v.reshape(32, 128)
-            return acc + jnp.sum(v * v, axis=0)
-
-        squares = lax.fori_loop(0, 250, step, totals[0], unroll=10)
-        last = rows[pl.ds(8000, 4), :].astype(F32) * m4
-        into[pl.ds(8000, 4), :] = last
-        totals[0] = squares + jnp.concatenate([last * last, jnp.zeros((4, 128), F32)], axis=0)
-        totals[1] = totals[1] + m8
-
-    def turn(i):
-        cb = order[i]
-        source = flat.at[max(i - 1, 0)]
-
-        def step(j, carry):
-            lags = pl.ds(pl.multiple_of(j * 128, 128), 128)
-            for d in range(4):
-                t = source[pl.ds(pl.multiple_of(j * 512, 512) + d, 128, stride=4), :]
-                t = t.astype(BF).T.reshape(4, 4, 8, 128)
-                for c in range(2):
-                    xr[c, cb, :, d, :, lags] = t[:, c]
-                for c in range(2, 4):
-                    for q in range(4):
-                        xr[c, q, cb, d, :, lags] = t[q, c]
-            return carry
-
-        lax.fori_loop(0, 16, step, 0, unroll=2)
+    def raw_block(c, a):
+        return remote(xr.at[c, a], r1.at[c, 0], a_s.at[c], a_r.at[c], at_first(c, firsts[c][1]))
+
+    def raw_piece(c, a, b):
+        return remote(xr.at[c, a, b], r1.at[c, 0, b], a_s.at[c], a_r.at[c], at_first(c, firsts[c][1]))
+
+    def second_order(c):
+        v, q1, q2, v2 = seconds[c]
+        return (v2, q1, q2, v)
+
+    def raw_second(c, k):
+        source = xr.at[c, firsts[c][1], second_order(c)[k]]
+        return remote(source, r1.at[c, 1, k], g_s.at[c, k], g_r.at[c, k], at_first(c, firsts[c][1]))
+
+    masks = []
+    for cb in order:
+        m4 = mask_ref[:, pl.ds(pl.multiple_of(cb * 128, 128), 128)].astype(F32)
+        masks.append(jnp.concatenate([m4, m4], axis=0))
+
+    def widen(i, j, acc):
+        rows = slab.at[i % 2].reshape(4 * WIDE, 128)
+        for r in range(16):
+            at = pl.ds(pl.multiple_of(j * 512, 512) + 32 * r, 32)
+            v = rows[at, :].astype(F32).reshape(4, 8, 128) * masks[i][None]
+            flat[max(i - 1, 0), at, :] = v.reshape(32, 128)
+            acc = acc + jnp.sum(v * v, axis=0)
+        return acc
+
+    def turn(i, j):
+        lags = pl.ds(pl.multiple_of(j * 128, 128), 128)
+        for d in range(4):
+            t = flat[max(i - 1, 0), pl.ds(pl.multiple_of(j * 512, 512) + d, 128, stride=4), :]
+            t = t.astype(BF).T.reshape(4, 4, 8, 128)
+            for c in range(2):
+                xr[c, order[i], :, d, :, lags] = t[:, c]
+            for c in range(2, 4):
+                for q in range(4):
+                    xr[c, q, order[i], d, :, lags] = t[q, c]
+
+    def send_raw(i):
         if i == 0:
             pl.semaphore_wait(barrier, len(neighbours) + len(peers))
             for c in range(2):
-                raw_block(c, 0, x2).start()
+                raw_block(c, x2).start()
         for c in range(2, 4):
-            raw_piece(c, 0, y2, cb).start()
-
-    widen(0)
-    turn(0)
-    widen(1)
-    widen(2)
-    widen(3)
-
-    en[0, 0] = totals[0]
-    en[0, 1] = totals[1]
-    energy_copies = [
-        remote(en.at[0], en.at[k], e_s.at[k], e_r.at[k], peers[k - 1]) for k in range(1, 8)
-    ]
-    for copy in energy_copies:
-        copy.start()
-    turn(1)
-    turn(2)
-    turn(3)
+            raw_piece(c, y2, order[i]).start()
+            if i == 0:
+                raw_second(c, 0).start()
 
     def tabulate(j, carry):
         lo = pltpu.roll(rows_ref[...], j * 16, 1)
@@ -154,7 +136,39 @@
             table[pl.ds(pl.multiple_of(a * 256 + j * 16, 16), 16), :] = both[:, 256 * (7 - a) : 256 * (7 - a) + WIDE]
         return carry
 
-    lax.fori_loop(0, 16, tabulate, 0)
+    lax.fori_loop(0, EARLY, tabulate, 0)
+
+    squares = jnp.zeros((8, 128), F32)
+    for q in range(4):
+        first_loads[q].wait()
+        squares = lax.fori_loop(4 * q, 4 * q + 4, lambda j, acc: widen(0, j, acc), squares)
+    def turn_all(i):
+        def step(j, carry):
+            turn(i, j)
+            return carry
+
+        lax.fori_loop(0, 16, step, 0, unroll=2)
+        send_raw(i)
+
+    turn_all(0)
+    for i in range(1, 4):
+        loads[i].wait()
+        if i < 3:
+            loads[i + 1].start()
+        squares = lax.fori_loop(0, 16, lambda j, acc, i=i: widen(i, j, acc), squares)
+
+    en[0, 0] = squares
+    en[0, 1] = masks[0] + masks[1] + masks[2] + masks[3]
+    energy_copies = [
+        remote(en.at[0], en.at[k], e_s.at[k], e_r.at[k], peers[k - 1]) for k in range(1, 8)
+    ]
+    for copy in energy_copies:
+        copy.start()
+
+    for i in range(1, 4):
+        turn_all(i)
+
+    lax.fori_loop(EARLY, 16, tabulate, 0)
 
     for copy in energy_copies:
         copy.wait_recv()
@@ -172,32 +186,44 @@
     weight_copies = [remote(ww, wn.at[k], w_s.at[k], w_r.at[k], neighbours[k]) for k in range(4)]
     for copy in weight_copies:
         copy.start()
-    for c in range(4):
-        raw_block(c, 1, firsts[c][1]).start()
+    for k in range(4):
+        for c in range(4 if k else 2):
+            raw_second(c, k).start()
 
     def scale_up(c):
         reach = jnp.maximum(jnp.max(ww[2], axis=0), jnp.max(wn[c, 2], axis=0))
-        units = jnp.stack([reach, jnp.minimum(1.0, 2.0 * reach)]) * 2.0**-12.5
+        units = jnp.stack([reach, jnp.minimum(1.0, 2.0 * reach)]) * 2.0**-9.6
         unit[c] = jnp.maximum(units, 1e-30).astype(BF).astype(F32)
 
     def code(v, u):
         t = v * (1.0 / u)
-        t = t * t
-        t = t * t
-        t = t * t
+        t2 = t * t
+        t4 = t2 * t2
+        t = t4 * t4 * t2
         return jnp.where(v < 0.0, -t, t)
+
+    def root(y, last, power):
+        units = last[..., 127:128]
+        size = jnp.exp((1.0 / power) * jnp.log(jnp.abs(y))) * units
+        return jnp.where(y < 0.0, -size, size)
 
     def decode(ref):
         y = ref[...].astype(F32)
-        size = jnp.exp(0.125 * jnp.log(jnp.abs(y))) * y_unit(ref)
-        return jnp.where(y < 0.0, -size, size)
-
-    def y_unit(ref):
-        return ref[:, :, WIDE - 1 : WIDE].astype(F32)
-
-    def second_order(c):
-        v, q1, q2, v2 = seconds[c]
-        return (v2, q1, q2, v)
+        return root(y, y[:, :, WIDE - 128 :], 10)
+
+    def code_whole(v):
+        largest = jnp.max(jnp.max(jnp.abs(v), axis=2, keepdims=True), axis=1, keepdims=True)
+        u = (jnp.maximum(largest, 1e-30) * 2.0**-10.4).astype(BF).astype(F32)
+        t = v * (1.0 / u)
+        t2 = t * t
+        t4 = t2 * t2
+        t = t4 * t4 * t4
+        lane = lax.broadcasted_iota(jnp.int32, (3, 8, WIDE), 2)
+        return jnp.where(lane == WIDE - 1, u, jnp.where(v < 0.0, -t, t)).astype(BF)
+
+    def decode_whole(ref):
+        y = ref[...].astype(F32)
+        return root(y, y[:, :, WIDE - 128 :], 12)
 
     def tile_sums(parts, slot, half, cols, sums):
         for at, raw, wq in parts:
@@ -218,13 +244,10 @@
 
         def before(self):
             if self.far:
-                if self.cs[0] == 0:
-                    for copy in weight_copies:
-                        copy.wait_recv()
-                    for c in range(4):
-                        scale_up(c)
                 for c in self.cs:
-                    raw_block(c, 0, x).wait_recv()
+                    weight_copies[c].wait_recv()
+                    scale_up(c)
+                    raw_block(c, x).wait_recv()
 
         def rows(self, c):
             return r1.at[c, 0] if self.far else xr.at[c, firsts[c][2]]
@@ -253,7 +276,7 @@
         def after(self):
             if self.far:
                 for c in self.cs:
-                    for k in range(4):
+                    for k in range(2):
                         sums_first(c, k).start()
 
     class SecondSums:
@@ -261,13 +284,14 @@
             self.k = k
 
         def before(self):
-            if self.k == 0:
-                for c in range(4):
-                    raw_block(c, 1, x).wait_recv()
+            for c in range(4):
+                raw_second(c, self.k).wait_recv()
+                if self.k == 3:
+                    sums_first(c, self.k).wait_recv()
 
         def rows(self, c):
             b = second_order(c)[self.k]
-            return xr.at[c, firsts[c][0], b], r1.at[c, 1, b]
+            return xr.at[c, firsts[c][0], b], r1.at[c, 1, self.k]
 
         def left(self):
             return [r[...].reshape(32, WIDE) for c in range(4) for r in self.rows(c)]
@@ -277,13 +301,22 @@
                 own, far = self.rows(c)
                 for half, cols in halves(n):
                     parts = [(c * 64, own, ww), (c * 64 + 32, far, wn.at[c])]
-                    sums = tile_sums(parts, slot, half, cols, [jnp.zeros((8, 128), F32)] * 3)
+                    if self.k == 3:
+                        last = pl.ds(WIDE - 128, 128)
+                        sums = [root(r2[c, self.k, k, :, cols].astype(F32), r2[c, self.k, k, :, last].astype(F32), 10) for k in range(3)]
+                    else:
+                        sums = [jnp.zeros((8, 128), F32)] * 3
+                    sums = tile_sums(parts, slot, half, cols, sums)
                     for k in range(3):
                         s2[c, self.k, k, :, cols] = sums[k]
 
         def after(self):
             for c in range(4):
                 (stage_three, stage_three, stage_four, finish)[self.k](c, self.k)
+            if self.k == 0:
+                for k in range(2, 4):
+                    for c in range(4):
+                        sums_first(c, k).start()
 
     def matmul(job, n, slot):
         cols = pl.ds(pl.multiple_of(n * 256, 256), 256)
@@ -295,27 +328,26 @@
         return remote(coded.at[c, b], r2.at[c, k], b_s.at[c, k], b_r.at[c, k], at_first(c, firsts[c][2]))
 
     def sums_second(c, k):
-        return remote(s2.at[c, k], r3.at[c, k], c_s.at[c, k], c_r.at[c, k], at_second(c, seconds[c][1]))
+        return remote(third.at[c, k], r3.at[c, k], c_s.at[c, k], c_r.at[c, k], at_second(c, seconds[c][1]))
 
     def sums_third(c):
-        return remote(s2.at[c, 2], r4.at[c], d_s.at[c], d_r.at[c], at_second(c, seconds[c][2]))
+        return remote(third.at[c, 2], r4.at[c], d_s.at[c], d_r.at[c], at_second(c, seconds[c][2]))
 
     def stage_three(c, k):
         sums_first(c, k).wait_recv()
-        s2[c, k] = s2[c, k] + decode(r2.at[c, k])
+        third[c, k] = code_whole(s2[c, k] + decode(r2.at[c, k]))
         sums_second(c, k).start()
 
     def stage_four(c, k):
         sums_first(c, 2).wait_recv()
         sums_second(c, 0).wait_recv()
-        s2[c, 2] = s2[c, 2] + decode(r2.at[c, 2]) + r3[c, 0]
+        third[c, 2] = code_whole(s2[c, 2] + decode(r2.at[c, 2]) + decode_whole(r3.at[c, 0]))
         sums_third(c).start()
 
     def finish(c, k):
-        sums_first(c, 3).wait_recv()
         sums_second(c, 1).wait_recv()
         sums_third(c).wait_recv()
-        total = s2[c, 3] + decode(r2.at[c, 3]) + r3[c, 1] + r4[c]
+        total = s2[c, 3] + decode_whole(r3.at[c, 1]) + decode_whole(r4.at[c])
         n = counts_column[8 * c : 8 * c + 8]
         sums_ref[0, pl.ds(8 * c, 8), :] = (total[0] / n)[:, :LAGS]
         sums_ref[1, pl.ds(8 * c, 8), :] = ((total[1] * total[1] + total[2] * total[2]) / (n * n))[:, :LAGS]
@@ -349,9 +381,9 @@
     for copy in energy_copies + weight_copies:
         copy.wait_send()
     for c in range(4):
-        for g in range(2):
-            raw_block(c, g, x).wait_send()
+        raw_block(c, x).wait_send()
         for k in range(4):
+            raw_second(c, k).wait_send()
             sums_first(c, k).wait_send()
         for k in range(2):
             sums_second(c, k).wait_send()
@@ -364,11 +396,11 @@
     dma = pltpu.SemaphoreType.DMA
     linear, coherence = pl.pallas_call(
         kernel,
-        out_shape=jax.ShapeDtypeStruct((2, 32, LAGS), F32),
+        out_shape=pltpu.VMEM((2, 32, LAGS), F32),
         in_specs=[pl.BlockSpec(memory_space=pl.ANY), vmem, vmem],
         out_specs=vmem,
         scratch_shapes=[
-            pltpu.VMEM((4, LAGS, 4, 128), BF),
+            pltpu.VMEM((2, WIDE, 4, 128), BF),
             pltpu.VMEM((3, 8192, 128), F32),
             pltpu.VMEM((4, 4, 4, 4, 8, WIDE), BF),
             pltpu.VMEM((4, 2, 4, 4, 8, WIDE), BF),
@@ -377,16 +409,18 @@
             pltpu.VMEM((4, 4, 3, 8, WIDE), F32),
             pltpu.VMEM((4, 4, 3, 8, WIDE), BF),
             pltpu.VMEM((4, 4, 3, 8, WIDE), BF),
-            pltpu.VMEM((4, 2, 3, 8, WIDE), F32),
-            pltpu.VMEM((4, 3, 8, WIDE), F32),
+            pltpu.VMEM((4, 3, 3, 8, WIDE), BF),
+            pltpu.VMEM((4, 2, 3, 8, WIDE), BF),
+            pltpu.VMEM((4, 3, 8, WIDE), BF),
             pltpu.VMEM((8, 2, 8, 128), F32),
             pltpu.VMEM((3, 4, 8, 128), F32),
             pltpu.VMEM((4, 3, 4, 8, 128), F32),
             pltpu.VMEM((4, 2, 8, 128), F32),
             pltpu.VMEM((2, 256, 256), F32),
             pltpu.VMEM((8, 4096), F32),
-            dma((4,)),
-            dma((4, 2)), dma((4, 2)),
+            dma((7,)),
+            dma((4,)), dma((4,)),
+            dma((4, 4)), dma((4, 4)),
             dma((4, 4)), dma((4, 4)),
             dma((4, 2)), dma((4, 2)),
             dma((4,)), dma((4,)),

time: 63.5 us -> 56.3 us (0.89)
  Pallas kernels: 60.8 us -> 54.6 us
  other arithmetic: 1.85 us -> 0.82 us
    pallas_call x1, Pallas kernels: 60.8 us -> 54.6 us  [shards(): pl.pallas_call(kernel, out_shape=pltpu.VMEM((2, 32, LAGS), F32), in_specs...]
    mul x1, other arithmetic: 1.85 us -> 0.82 us  [shards(): return (linear * coherence, linear)]
where the time goes in v4:
time: 56.3 us; the launch traced here: 56.1 us
  Pallas kernels  54.6 us (97%)
  other arithmetic  0.82 us (1%)
  between operations  0.64 us (1%)
    pallas_call x1, Pallas kernels, shards(): pl.pallas_call(kernel, out_shape=pltpu.VMEM((2, 32, LAGS), F32), in_specs...  54.6 us

profile of v4, /device:TPU:0, one launch (start us, length us, event | category | flops | bytes accessed | tf_op | source)
XLA Modules:
  0.0 56.1 jit_solution(1930094227140217011)
XLA Ops:
  0.6 54.6 %shard_map.50 = f32[2,32,2001]{2,1,0:T(8,128)S(1)} custom-call(bf16[2001,4,512]{2,1,0:T(4,128)(2,1)} %bitcast.7, s32[4,512]{1,0:T(4,128)} %mask_ref.1, s32[1,32]{1,0:T(1,128)} %bitcast.8), custom_call_target="tpu_custom_call" | custom-call | tf_op jit(solution)/shard_map/pallas_call | solution.py:397
  55.2 0.8 %bitcast_multiply_fusion = (f32[32,2001]{1,0:T(8,128)}, f32[32,2001]{1,0:T(8,128)}) fusion(f32[2,32,2001]{2,1,0:T(8,128)S(1)} %shard_map.50), kind=kLoop, calls=%fused_computation | loop fusion | flops 64032 | bytes 1024512 | tf_op jit(solution)/shard_map/mul | solution.py:434

commit v5 on v4

--- a/solution.py
+++ b/solution.py
@@ -100,9 +100,10 @@
 
     def widen(i, j, acc):
         rows = slab.at[i % 2].reshape(4 * WIDE, 128)
+        narrow = jnp.concatenate([masks[i]] * 4, axis=0).astype(BF)
         for r in range(16):
             at = pl.ds(pl.multiple_of(j * 512, 512) + 32 * r, 32)
-            v = rows[at, :].astype(F32).reshape(4, 8, 128) * masks[i][None]
+            v = (rows[at, :] * narrow).astype(F32).reshape(4, 8, 128)
             flat[max(i - 1, 0), at, :] = v.reshape(32, 128)
             acc = acc + jnp.sum(v * v, axis=0)
         return acc
@@ -193,10 +194,12 @@
     def scale_up(c):
         reach = jnp.maximum(jnp.max(ww[2], axis=0), jnp.max(wn[c, 2], axis=0))
         units = jnp.stack([reach, jnp.minimum(1.0, 2.0 * reach)]) * 2.0**-9.6
-        unit[c] = jnp.maximum(units, 1e-30).astype(BF).astype(F32)
-
-    def code(v, u):
-        t = v * (1.0 / u)
+        units = jnp.maximum(units, 1e-30).astype(BF).astype(F32)
+        unit[c, 0] = units
+        unit[c, 1] = 1.0 / units
+
+    def code(v, inverse_unit):
+        t = v * inverse_unit
         t2 = t * t
         t4 = t2 * t2
         t = t4 * t4 * t2
@@ -266,11 +269,10 @@
                             if not self.far:
                                 s1[c, b, k, :, cols] = sums[k]
                                 continue
-                            u = unit[c, min(k, 1)]
-                            y = code(sums[k], u)
+                            y = code(sums[k], unit[c, 1, min(k, 1)])
                             if isinstance(n, int) and n == 7 and half == 1:
                                 lane = lax.broadcasted_iota(jnp.int32, (8, 128), 1)
-                                y = jnp.where(lane == 127, u, y)
+                                y = jnp.where(lane == 127, unit[c, 0, min(k, 1)], y)
                             coded[c, b, k, :, cols] = y.astype(BF)
 
         def after(self):
@@ -311,17 +313,22 @@
                         s2[c, self.k, k, :, cols] = sums[k]
 
         def after(self):
-            for c in range(4):
-                (stage_three, stage_three, stage_four, finish)[self.k](c, self.k)
             if self.k == 0:
                 for k in range(2, 4):
                     for c in range(4):
                         sums_first(c, k).start()
+            elif self.k == 1:
+                for k in range(2):
+                    for c in range(4):
+                        stage_three(c, k)
+            else:
+                for c in range(4):
+                    (stage_four, finish)[self.k - 2](c, self.k)
 
     def matmul(job, n, slot):
         cols = pl.ds(pl.multiple_of(n * 256, 256), 256)
         lhs = jnp.concatenate(job.left(), axis=0)
-        hil[slot] = jnp.dot(lhs, table[:, cols], preferred_element_type=F32)
+        hil[slot, : lhs.shape[0]] = jnp.dot(lhs, table[:, cols], preferred_element_type=F32)
 
     def sums_first(c, k):
         b = second_order(c)[k]
@@ -356,7 +363,7 @@
     across = lax.broadcasted_iota(jnp.int32, (32, 32), 0) == lax.broadcasted_iota(jnp.int32, (32, 32), 1)
     counts_column = jnp.sum(jnp.where(across, counts, 0.0), axis=1, keepdims=True)
 
-    jobs = [FirstSums(cs, far) for far in (False, True) for cs in ((0, 1), (2, 3))]
+    jobs = [FirstSums((0, 1, 2, 3), False), FirstSums((0, 1), True), FirstSums((2, 3), True)]
     jobs += [SecondSums(k) for k in range(4)]
     matmul(jobs[0], 0, 0)
     for job, following in zip(jobs, jobs[1:] + [None]):
@@ -415,8 +422,8 @@
             pltpu.VMEM((8, 2, 8, 128), F32),
             pltpu.VMEM((3, 4, 8, 128), F32),
             pltpu.VMEM((4, 3, 4, 8, 128), F32),
-            pltpu.VMEM((4, 2, 8, 128), F32),
-            pltpu.VMEM((2, 256, 256), F32),
+            pltpu.VMEM((4, 2, 2, 8, 128), F32),
+            pltpu.VMEM((2, 512, 256), F32),
             pltpu.VMEM((8, 4096), F32),
             dma((7,)),
             dma((4,)), dma((4,)),

time: 56.3 us -> 54.1 us (0.961)
  Pallas kernels: 54.6 us -> 52.4 us
    pallas_call x1, Pallas kernels: 54.6 us -> 52.4 us  [shards(): pl.pallas_call(kernel, out_shape=pltpu.VMEM((2, 32, LAGS), F32), in_specs...]
where the time goes in v5:
time: 54.1 us; the launch traced here: 53.9 us
  Pallas kernels  52.4 us (97%)
  other arithmetic  0.82 us (2%)
  between operations  0.64 us (1%)
    pallas_call x1, Pallas kernels, shards(): pl.pallas_call(kernel, out_shape=pltpu.VMEM((2, 32, LAGS), F32), in_specs...  52.4 us

profile of v5, /device:TPU:0, one launch (start us, length us, event | category | flops | bytes accessed | tf_op | source)
XLA Modules:
  0.0 53.9 jit_solution(16260138707056626784)
XLA Ops:
  0.6 52.4 %shard_map.50 = f32[2,32,2001]{2,1,0:T(8,128)S(1)} custom-call(bf16[2001,4,512]{2,1,0:T(4,128)(2,1)} %bitcast.7, s32[4,512]{1,0:T(4,128)} %mask_ref.1, s32[1,32]{1,0:T(1,128)} %bitcast.8), custom_call_target="tpu_custom_call" | custom-call | tf_op jit(solution)/shard_map/pallas_call | solution.py:404
  53.1 0.8 %bitcast_multiply_fusion = (f32[32,2001]{1,0:T(8,128)}, f32[32,2001]{1,0:T(8,128)}) fusion(f32[2,32,2001]{2,1,0:T(8,128)S(1)} %shard_map.50), kind=kLoop, calls=%fused_computation | loop fusion | flops 64032 | bytes 1024512 | tf_op jit(solution)/shard_map/mul | solution.py:441
